TPU v7x, 32 devices: a whole 2x2x4 slice. The times are simulated.
32 devices in a mesh: dp: 16 (over z, y, x), rep: 2 (over core).
Axes of the slice: x: 2, y: 2, z: 4, core: 2. Of those that a mesh axis runs over, the one named last changes fastest.
Arguments:
- ids: int32 [8192], P(('dp', 'rep')), may hold values from 0 to 65520
- counts: int32 [32], P(('dp', 'rep')), may hold values from 1 to 256, as said below
- hash_scale: int32 [512], replicated, may hold values from 1 to 32767
- hash_shift: int32 [512], replicated, may hold values from 0 to 65520
- w_code: bfloat16 [512, 1024], replicated, may hold values from -0.25 to 0.25
- norm_gain: float32 [1024], replicated, may hold values from 0.5 to 1.5
- norm_bias: float32 [1024], replicated, may hold values from -3 to 3
- w_out: bfloat16 [1024, 128], replicated, may hold values from -0.1875 to 0.1875
- out_bias: float32 [128], replicated, may hold values from -3 to 3
- cotangent: bfloat16 [8192, 128], P(('dp', 'rep')), may hold values from -6 to 6
Outputs:
- embeddings: bfloat16 [8192, 128], P(('dp', 'rep'))
- grad_code_t: float32 [1024, 512], P(('dp', 'rep'))
- grad_out: float32 [1024, 128], P(('dp', 'rep'))
- grad_gain: float32 [1024], replicated
- grad_bias: float32 [1024], replicated
Inputs may be any that keep to these rules, and one draw needn't show every extreme that they name: Each device has 1 to 256 live slots, the first ones of its slots; the counts of the devices of one rep index sum to exactly 1024, and in each such group one device has exactly 256.
All inputs are finite; a program needn't handle non-finite values.
Results may differ from a plain program's by a relative error of at most 0.006.
Values may be sent and summed in bfloat16 or wider, within the bound.
No kernel may reach another device: no remote copies, remote signals or barrier semaphores. Data moves between devices by JAX's collectives and lax.ppermute only.
A program may use at most 64 MiB of HBM per device.

v0:
```python
import math
import jax
import jax.numpy as jnp
from jax import lax
from jax.sharding import PartitionSpec as P

BLOCK = 256
modulus = 65521
epsilon = 1e-05


def hashed(ident, hash_scale, hash_shift):
    resid = ident % modulus
    bucket = (hash_scale[None, :] * resid[:, None] + hash_shift[None, :]) % modulus
    return (bucket.astype(jnp.float32) * (2.0 / (modulus - 1)) - 1.0).astype(jnp.bfloat16)


def mish_parts(gated):
    softer = jax.nn.softplus(gated)
    tangent = jnp.tanh(softer)
    return (gated * tangent, tangent + gated * (1.0 - tangent * tangent) * jax.nn.sigmoid(gated))


def owner_rows(dpre_rows, row_ids, hash_scale, hash_shift):
    dp_count = lax.axis_size("dp")
    rep_count = lax.axis_size("rep")
    device_count = dp_count * rep_count
    row_count = dpre_rows.shape[0]
    columns = lax.all_to_all(
        lax.all_to_all(dpre_rows, "dp", split_axis=1, concat_axis=0, tiled=True),
        "rep",
        split_axis=1,
        concat_axis=0,
        tiled=True,
    )
    everyone = lax.all_gather(row_ids, ("dp", "rep"), axis=0, tiled=True)
    everyone = everyone.reshape(dp_count, rep_count, row_count).transpose(1, 0, 2).reshape(-1)
    group = math.gcd(device_count, max(1, 8192 // row_count))
    step_rows = group * row_count

    def accumulate(index, grad_rows):
        start = index * step_rows
        id_block = lax.dynamic_slice_in_dim(everyone, start, step_rows, 0)
        col_block = lax.dynamic_slice_in_dim(columns, start, step_rows, 0)
        code_block = hashed(id_block, hash_scale, hash_shift)
        return grad_rows + lax.dot_general(
            col_block, code_block, (((0,), (0,)), ((), ())), preferred_element_type=jnp.float32
        )

    start_rows = jnp.zeros((columns.shape[1], hash_scale.shape[0]), jnp.float32)
    return lax.fori_loop(0, device_count // group, accumulate, start_rows)


def train_rows(
    code_rows,
    cot_rows,
    live_count,
    row_ids,
    hash_scale,
    hash_shift,
    w_code,
    norm_gain,
    norm_bias,
    w_out,
    out_bias,
):
    row_count = code_rows.shape[0]
    hidden = w_code.shape[1]
    width = w_out.shape[1]
    live_flags = jnp.arange(row_count, dtype=jnp.int32) < live_count
    block_total = (live_count + BLOCK - 1) // BLOCK
    zero_row = jnp.zeros((hidden,), jnp.float32)

    def first_pass(block_index, state_carry):
        stored, sum_hidden, sum_square = state_carry
        keep_rows = live_flags[:, None]
        preact = jnp.dot(code_rows, w_code, preferred_element_type=jnp.float32)
        masked = jnp.where(keep_rows, preact, 0.0)
        stored = preact
        return (stored, sum_hidden + masked.sum(0), sum_square + (masked * masked).sum(0))

    stored, sum_hidden, sum_square = lax.fori_loop(
        0,
        block_total,
        first_pass,
        (jnp.zeros((row_count, hidden), jnp.float32), zero_row, zero_row),
    )
    sum_hidden, sum_square, total = lax.psum(
        (sum_hidden, sum_square, live_count.astype(jnp.float32)), ("dp", "rep")
    )
    feature_mean = sum_hidden / total
    inv_std = lax.rsqrt(sum_square / total - feature_mean * feature_mean + epsilon)
    loss_scale = lax.rsqrt(total)

    def second_pass(block_index, state_carry):
        stored, dvalue_rows, embedded, grad_gain, grad_bias, grad_out = state_carry
        keep_rows = live_flags[:, None]
        normed = (stored - feature_mean) * inv_std
        act_full, mish_slope = mish_parts(normed * norm_gain + norm_bias)
        activation = act_full.astype(jnp.bfloat16)
        out_rows = jnp.dot(activation, w_out, preferred_element_type=jnp.float32) + out_bias
        out_rows = jnp.where(keep_rows, out_rows, 0.0).astype(jnp.bfloat16)
        delta_rows = jnp.where(keep_rows, cot_rows.astype(jnp.float32) * loss_scale, 0.0).astype(
            jnp.bfloat16
        )
        grad_act = lax.dot_general(
            delta_rows, w_out, (((1,), (1,)), ((), ())), preferred_element_type=jnp.float32
        )
        dvalue = grad_act * mish_slope
        stored = normed
        dvalue_rows = dvalue
        embedded = out_rows
        out_part = lax.dot_general(
            activation, delta_rows, (((0,), (0,)), ((), ())), preferred_element_type=jnp.float32
        )
        return (
            stored,
            dvalue_rows,
            embedded,
            grad_gain + (dvalue * normed).sum(0),
            grad_bias + dvalue.sum(0),
            grad_out + out_part,
        )

    start_state = (
        stored,
        jnp.zeros((row_count, hidden), jnp.float32),
        jnp.zeros((row_count, width), jnp.bfloat16),
        zero_row,
        zero_row,
        jnp.zeros((hidden, width), jnp.float32),
    )
    stored, dvalue_rows, embedded, grad_gain, grad_bias, grad_out = lax.fori_loop(
        0, block_total, second_pass, start_state
    )
    grad_gain, grad_bias = lax.psum((grad_gain, grad_bias), ("dp", "rep"))

    def signal_block():
        keep_rows = live_flags[:, None]
        dpre = norm_gain * inv_std * (dvalue_rows - grad_bias / total - stored * grad_gain / total)
        return jnp.where(keep_rows, dpre, 0.0).astype(jnp.bfloat16)

    def store_pass(block_index, dpre_rows):
        return signal_block()

    dpre_rows = lax.fori_loop(
        0, block_total, store_pass, jnp.zeros((row_count, hidden), jnp.bfloat16)
    )
    out_share = lax.psum_scatter(grad_out, ("dp", "rep"), scatter_dimension=0, tiled=True)
    code_share = owner_rows(dpre_rows, row_ids, hash_scale, hash_shift)
    return (embedded, code_share, out_share, grad_gain, grad_bias)


def per_device(
    ids, counts, hash_scale, hash_shift, w_code, norm_gain, norm_bias, w_out, out_bias, cotangent
):
    live_count = counts[0]
    weights = (w_code, norm_gain, norm_bias, w_out, out_bias)
    code_rows = hashed(ids, hash_scale, hash_shift)
    embedded, code_share, out_share, grad_gain, grad_bias = train_rows(
        code_rows, cotangent, live_count, ids, hash_scale, hash_shift, *weights
    )
    return (embedded, code_share, out_share, grad_gain, grad_bias)


def solution(mesh):
    return jax.shard_map(
        per_device,
        mesh=mesh,
        in_specs=(
            P(("dp", "rep")),
            P(("dp", "rep")),
            P(),
            P(),
            P(),
            P(),
            P(),
            P(),
            P(),
            P(("dp", "rep"), None),
        ),
        out_specs=(
            P(("dp", "rep"), None),
            P(("dp", "rep"), None),
            P(("dp", "rep"), None),
            P(),
            P(),
        ),
        check_vma=False,
    )
```

profile of v0, /device:TPU:0, one launch (start us, length us, event | category | flops | bytes accessed | tf_op | source)
XLA Modules:
  0.0 264.1 jit_solution(4582363690425462505)
XLA Ops:
  7.2 0.0 copy-start
  7.9 0.7 and_select_fusion
  8.6 0.0 copy-done
  8.6 1.4 multiply_reduce_fusion.1
  10.1 1.1 broadcast.69.clone
  11.2 1.0 while.57
  11.2 1.0 copy.38
  12.2 0.0 copy-start.3
  12.3 0.0 copy-start.4
  12.3 0.0 copy-start.6
  12.3 0.0 copy-start.9
  12.3 42.2 %all-reduce.1 = (f32[1024]{0:T(1024)S(1)}, f32[]{:T(128)}, f32[1024]{0:T(1024)S(1)}) all-reduce(f32[1024]{0:T(1024)S(1)} %get-tuple-element.387, f32[]{:T(128)S(6)} %convert_element_type.36, f32[1024]{0:T(1024)S(1)} %get-tuple-element.388), channel_id=1, replica_groups=mesh['dp'=16,'rep'=2] {'dp','rep'}, use_global_device_ids=true, to_apply=%region_4.5 | all-reduce | flops 2049 | bytes 16392 | tf_op jit(solution)/shard_map/psum | solution.py:88
  55.2 0.0 copy-done.5
  55.2 0.7 fusion.43
  55.8 1.1 broadcast.69
  57.0 0.6 broadcast_in_dim.81
  57.6 0.0 copy-done.1
  57.6 0.0 copy-done.3
  57.6 0.0 copy-done.4
  57.6 5.0 %while.58 = (s32[]{:T(128)}, f32[256,1024]{1,0:T(8,128)S(1)}, f32[256,1024]{1,0:T(8,128)}, bf16[256,128]{1,0:T(8,128)(2,1)}, f32[1024]{0:T(1024)S(1)}, /*index=5...) while((s32[]{:T(128)}, f32[256,1024]{1,0:T(8,128)S(1)}, ...), condition=%wide.region_10.11_spmd.clone, body=%wide.region_7.10_spmd.clone.sunk | while | flops 210206976 | bytes 7595697 | solution.py:133
  57.7 0.8 multiply_convert_fusion.2
  58.4 0.7 iota_compare_fusion.5
  59.1 2.2 fusion.60
  61.3 0.4 convolution_add_fusion.3
  61.7 0.9 fusion.61
  62.7 40.3 %all-reduce = (f32[1024]{0:T(1024)S(1)}, f32[1024]{0:T(1024)S(1)}) all-reduce(f32[1024]{0:T(1024)S(1)} %get-tuple-element.390, f32[1024]{0:T(1024)S(1)} %get-tuple-element.392), channel_id=1, replica_groups=mesh['dp'=16,'rep'=2] {'dp','rep'}, use_global_device_ids=true, to_apply=%region_11.12 | all-reduce | flops 2048 | bytes 16384 | tf_op jit(solution)/shard_map/psum | solution.py:136
  103.0 0.8 broadcast_in_dim.83
  103.9 0.0 copy-done.2
  103.9 4.2 %while.59 = (s32[]{:T(128)}, bf16[256,1024]{1,0:T(8,128)(2,1)}, s32[]{:T(128)}, f32[1,1024]{1,0:T(1,128)S(1)}, f32[]{:T(128)}, /*index=5*/f32[1024]{0:T(1024)S(1...) while((s32[]{:T(128)}, bf16[256,1024]{1,0:T(8,128)(2,1)}, ...), condition=%wide.region_14.15_spmd.clone, body=%wide.region_13.14_spmd.clone.sunk | while | flops 1836290 | bytes 2642553 | solution.py:146
  103.9 0.6 broadcast_divide_fusion.3
  104.5 0.7 iota_compare_fusion.6
  105.2 2.9 %select_convert_fusion.7 = bf16[256,1024]{1,0:T(8,128)(2,1)} fusion(f32[256,1024]{1,0:T(8,128)S(1)} %get-tuple-element.870, f32[256,1024]{1,0:T(8,128)} %get-tuple-element.868, f32[]{:T(128)} %get-tuple-element.866, f32[1024]{0:T(1024)S(1)} %get-tuple-element.869, f32[1024]{0:T(1024)S(1)} %broadcast_divide_fusion.3, f32[1024]{0:T(1024)S(1)} %bitcast.37, ...), kind=kLoop, calls=%fused_computation.18.clone.1 | loop fusion | flops 1835008 | bytes 2633988 | tf_op jit(solution)/shard_map/while/body/convert_element_type | solution.py:141
  108.1 2.0 copy.22
  110.1 6.4 %all-to-all-start = ((bf16[256,16,64]{0,2,1:T(8,128)(2,1)}), bf16[256,16,64]{0,2,1:T(8,128)(2,1)S(1)}, u32[]{:S(2)}, u32[]{:S(2)}) async-start(bf16[256,16,64]{0,2,1:T(8,128)(2,1)} %bitcast.2), calls=%async_computation | async-start | bytes 1048576 | tf_op jit(solution)/shard_map/all_to_all | solution.py:30
  116.5 0.0 reduce-scatter.2.cloned.1.call-start
  116.6 0.7 reduce-scatter.2.cloned.1.call-update
  117.3 41.9 %all-gather = s32[32,1,256]{2,1,0:T(1,128)S(1)} all-gather(s32[1,1,256]{2,1,0:T(1,128)S(1)} %bitcast.41), channel_id=1, replica_groups=mesh['dp'=16,'rep'=2] {'dp','rep'}, dimensions={0}, use_global_device_ids=true | all-gather | bytes 33792 | tf_op jit(solution)/shard_map/all_gather | solution.py:36
  159.2 0.2 remainder_reduce_fusion
  159.4 0.0 all-to-all-done
  159.4 0.3 copy.23
  159.7 0.2 all_to_all.29
  160.0 0.0 copy-start.11
  160.0 0.0 copy-start.12
  160.0 4.2 %all_to_all.35 = bf16[4096,2,32]{0,2,1:T(8,128)(2,1)S(1)} all-to-all(bf16[4096,2,32]{0,2,1:T(8,128)(2,1)S(1)} %all_to_all.29), channel_id=1, replica_groups=mesh['dp'=16,'rep'=2] {'rep'}, dimensions={1} | all-to-all | bytes 1048576 | tf_op jit(solution)/shard_map/all_to_all | solution.py:29
  164.2 0.0 copy-done.11
  164.2 0.0 copy-done.12
  164.2 11.9 %fusion.16 = f32[32,512]{1,0:T(8,128)} fusion(bf16[8192,32]{0,1:T(8,128)(2,1)S(1)} %bitcast.35, s32[512]{0:T(512)S(1)} %copy-done.11, s32[8192]{0:T(1024)S(1)} %add_select_fusion.2, s32[512]{0:T(512)S(1)} %copy-done.12), kind=kOutput, calls=%fused_computation.30 | convolution fusion | flops 318767104 | bytes 626688 | tf_op jit(solution)/shard_map/while/body/eval_jaxpr/dot_general | solution.py:46
  176.1 81.1 %reduce-scatter.2.cloned.1.call-done = f32[32,128]{1,0:T(8,128)} async-done(((f32[1024,128]{1,0:T(8,128)}), f32[32,128]{1,0:T(8,128)}) %reduce-scatter.2.cloned.1.call-update) | async-done | bytes 16400 | tf_op jit(solution)/shard_map/reduce_scatter | solution.py:149
  (26 shorter events, 0.2 us)
Async XLA Ops:
  7.2 1.5 copy-start
  11.2 43.9 %copy-start.5 = (f32[1024]{0:T(1024)S(1)}, f32[1024]{0:T(1024)}, u32[]{:S(2)}) copy-start(f32[1024]{0:T(1024)} %param.21) | copy-start | bytes 12292
  12.2 45.4 %copy-start.1 = (f32[256,1024]{1,0:T(8,128)S(1)}, f32[256,1024]{1,0:T(8,128)}, u32[]{:S(2)}) copy-start(f32[256,1024]{1,0:T(8,128)} %get-tuple-element.787) | copy-start | bytes 3145732
  12.2 45.4 %copy-start.3 = (bf16[1024,128]{1,0:T(8,128)(2,1)S(1)}, bf16[1024,128]{1,0:T(8,128)(2,1)}, u32[]{:S(2)}) copy-start(bf16[1024,128]{1,0:T(8,128)(2,1)} %param.23) | copy-start | bytes 786436
  12.3 45.3 %copy-start.4 = (bf16[256,128]{1,0:T(8,128)(2,1)S(1)}, bf16[256,128]{1,0:T(8,128)(2,1)}, u32[]{:S(2)}) copy-start(bf16[256,128]{1,0:T(8,128)(2,1)} %param.25) | copy-start | bytes 196612
  12.3 45.3 %copy-start.6 = (f32[1024]{0:T(1024)S(1)}, f32[1024]{0:T(1024)}, u32[]{:S(2)}) copy-start(f32[1024]{0:T(1024)} %param.22) | copy-start | bytes 12292
  12.3 45.3 %copy-start.9 = (f32[128]{0:T(128)S(1)}, f32[128]{0:T(128)}, u32[]{:S(2)}) copy-start(f32[128]{0:T(128)} %param.24) | copy-start | bytes 1540
  62.7 41.2 %copy-start.2 = (f32[1024,128]{1,0:T(8,128)}, f32[1024,128]{1,0:T(8,128)S(1)}, u32[]{:S(2)}) copy-start(f32[1024,128]{1,0:T(8,128)S(1)} %get-tuple-element.395) | copy-start | bytes 1572868
  108.1 2.0 copy-start.7
  108.1 2.1 copy-start.8
  110.1 7.1 %copy-start.10 = (s32[256]{0:T(256)S(1)}, s32[256]{0:T(256)}, u32[]{:S(2)}) copy-start(s32[256]{0:T(256)} %param.16) | copy-start | bytes 3076
  110.1 49.3 %all-to-all-start = ((bf16[256,16,64]{0,2,1:T(8,128)(2,1)}), bf16[256,16,64]{0,2,1:T(8,128)(2,1)S(1)}, u32[]{:S(2)}, u32[]{:S(2)}) async-start(bf16[256,16,64]{0,2,1:T(8,128)(2,1)} %bitcast.2), calls=%async_computation | async-start | bytes 1048576 | tf_op jit(solution)/shard_map/all_to_all | solution.py:30
  116.5 140.7 %reduce-scatter.2.cloned.1.call-start = ((), (), s32[]{:S(2)}) async-start(), calls=%async_computation.3 | async-start | bytes 540672 | tf_op jit(solution)/shard_map/reduce_scatter | solution.py:149
  160.0 4.2 %copy-start.11 = (s32[512]{0:T(512)S(1)}, s32[512]{0:T(512)}, u32[]{:S(2)}) copy-start(s32[512]{0:T(512)} %param.19) | copy-start | bytes 6148
  160.0 4.2 %copy-start.12 = (s32[512]{0:T(512)S(1)}, s32[512]{0:T(512)}, u32[]{:S(2)}) copy-start(s32[512]{0:T(512)} %param.18) | copy-start | bytes 6148
Sparse Core Ops, SparseCore 0:
  120.1 137.0 reduce-scatter.1
where the time goes:
time: 265 us; the launch traced here: 264 us
  blocking collectives  129 us (49%)
  waiting for transfers between devices  81.8 us (31%)
  matrix products  16.9 us (6%)
  between operations  15.7 us (6%)
  local copies, waits for them, and re-layouts  7.5 us (3%)
  other arithmetic  7.18 us (3%)
  starting transfers between devices  6.41 us (2%)
    reduce_scatter x1, waiting for transfers between devices, train_rows(): lax.psum_scatter(grad_out, ('dp', 'rep'), scatter_dimension=0, tiled=True)  81.1 us
    psum x1, blocking collectives, train_rows(): lax.psum((sum_hidden, sum_square, live_count.astype(jnp.float32)), ('dp',...  42.2 us
    all_gather x1, blocking collectives, owner_rows(): everyone = lax.all_gather(row_ids, ('dp', 'rep'), axis=0, tiled=True)  41.9 us
    psum x1, blocking collectives, train_rows(): grad_gain, grad_bias = lax.psum((grad_gain, grad_bias), ('dp', 'rep'))  40.3 us
    dot_general x1, matrix products, accumulate(): lax.dot_general(col_block, code_block, (((0,), (0,)), ((), ())), preferre...  11.9 us
    all_to_all x1, starting transfers between devices, owner_rows(): lax.all_to_all(dpre_rows, 'dp', split_axis=1, concat_axis=0, tiled=True)  6.37 us
  transfers between devices with their start and end apart: 2, of which 1 were waited for; matrix products, arithmetic and copies ran while one was open for 5% of the time, Pallas kernels for 0%

commit v1 on v0

--- a/solution.py
+++ b/solution.py
@@ -133,7 +133,11 @@
     stored, dvalue_rows, embedded, grad_gain, grad_bias, grad_out = lax.fori_loop(
         0, block_total, second_pass, start_state
     )
-    grad_gain, grad_bias = lax.psum((grad_gain, grad_bias), ("dp", "rep"))
+
+    def zones_enter(obj):
+        return lax.psum(lax.psum(obj, axis_name="rep"), axis_name="dp")
+
+    grad_gain, grad_bias = zones_enter((grad_gain, grad_bias))
 
     def signal_block():
         keep_rows = live_flags[:, None]

time: 265 us -> 265 us (level)
  blocking collectives: 129 us -> 132 us
  starting transfers between devices: 6.41 us -> 3.75 us
    psum x1 -> x2, blocking collectives: 40.3 us -> 43.6 us  [zones_enter(): return lax.psum(lax.psum(obj, axis_name='rep'), axis_name='dp')]
    all_to_all x1, starting transfers between devices: 6.37 us -> 3.71 us  [owner_rows(): lax.all_to_all(dpre_rows, 'dp', split_axis=1, concat_axis=0, tiled=True)]
where the time goes in v1:
time: 265 us
  blocking collectives  132 us (50%)
  waiting for transfers between devices  81.8 us (31%)
  matrix products  16.9 us (6%)
  between operations  15.7 us (6%)
  local copies, waits for them, and re-layouts  7.54 us (3%)
  other arithmetic  7.19 us (3%)
  starting transfers between devices  3.75 us (1%)
    reduce_scatter x1, waiting for transfers between devices, train_rows(): lax.psum_scatter(grad_out, ('dp', 'rep'), scatter_dimension=0, tiled=True)  81.1 us
    psum x2, blocking collectives, zones_enter(): return lax.psum(lax.psum(obj, axis_name='rep'), axis_name='dp')  43.6 us
    psum x1, blocking collectives, train_rows(): lax.psum((sum_hidden, sum_square, live_count.astype(jnp.float32)), ('dp',...  42.2 us
    all_gather x1, blocking collectives, owner_rows(): everyone = lax.all_gather(row_ids, ('dp', 'rep'), axis=0, tiled=True)  41.9 us
    dot_general x1, matrix products, accumulate(): lax.dot_general(col_block, code_block, (((0,), (0,)), ((), ())), preferre...  11.9 us
  transfers between devices with their start and end apart: 2, of which 1 were waited for; matrix products, arithmetic and copies ran while one was open for 5% of the time, Pallas kernels for 0%

profile of v1, /device:TPU:0, one launch (start us, length us, event | category | flops | bytes accessed | tf_op | source)
XLA Modules:
  0.0 264.8 jit_solution(12155949675315968485)
XLA Ops:
  7.2 0.0 copy-start
  7.9 0.7 and_select_fusion
  8.6 0.0 copy-done
  8.6 1.4 multiply_reduce_fusion.1
  10.1 1.1 broadcast.69.clone
  11.2 1.0 while.57
  11.2 1.0 copy.38
  12.3 0.0 copy-start.3
  12.3 0.0 copy-start.4
  12.3 0.0 copy-start.6
  12.3 0.0 copy-start.9
  12.3 42.2 %all-reduce = (f32[1024]{0:T(1024)S(1)}, f32[]{:T(128)}, f32[1024]{0:T(1024)S(1)}) all-reduce(f32[1024]{0:T(1024)S(1)} %get-tuple-element.387, f32[]{:T(128)S(6)} %convert_element_type.36, f32[1024]{0:T(1024)S(1)} %get-tuple-element.388), channel_id=1, replica_groups=mesh['dp'=16,'rep'=2] {'dp','rep'}, use_global_device_ids=true, to_apply=%region_4.5 | all-reduce | flops 2049 | bytes 16392 | tf_op jit(solution)/shard_map/psum | solution.py:88
  55.2 0.0 copy-done.5
  55.2 0.7 fusion.43
  55.9 1.1 broadcast.69
  57.0 0.6 broadcast_in_dim.81
  57.6 0.0 copy-done.1
  57.6 0.0 copy-done.3
  57.6 0.0 copy-done.4
  57.7 5.0 %while.58 = (s32[]{:T(128)}, f32[256,1024]{1,0:T(8,128)S(1)}, f32[256,1024]{1,0:T(8,128)}, bf16[256,128]{1,0:T(8,128)(2,1)}, f32[1024]{0:T(1024)S(1)}, /*index=5...) while((s32[]{:T(128)}, f32[256,1024]{1,0:T(8,128)S(1)}, ...), condition=%wide.region_10.11_spmd.clone, body=%wide.region_7.10_spmd.clone.sunk | while | flops 210206976 | bytes 7595697 | solution.py:133
  57.7 0.8 multiply_convert_fusion.2
  58.5 0.7 iota_compare_fusion.5
  59.1 2.2 fusion.60
  61.4 0.4 convolution_add_fusion.3
  61.8 0.9 fusion.61
  62.7 2.5 all-reduce.2
  65.2 41.1 %all-reduce.1 = (f32[1024]{0:T(1024)S(1)}, f32[1024]{0:T(1024)S(1)}) all-reduce(f32[1024]{0:T(1024)S(1)} %get-tuple-element.534, f32[1024]{0:T(1024)S(1)} %get-tuple-element.535), channel_id=1, replica_groups=mesh['dp'=16,'rep'=2] {'dp'}, use_global_device_ids=true, to_apply=%region_12.13 | all-reduce | flops 2048 | bytes 16384 | tf_op jit(solution)/shard_map/psum | solution.py:138
  106.3 0.9 broadcast_in_dim.83
  107.2 0.0 copy-done.2
  107.2 4.2 %while.59 = (s32[]{:T(128)}, bf16[256,1024]{1,0:T(8,128)(2,1)}, s32[]{:T(128)}, f32[1,1024]{1,0:T(1,128)S(1)}, f32[]{:T(128)}, /*index=5*/f32[1024]{0:T(1024)S(1...) while((s32[]{:T(128)}, bf16[256,1024]{1,0:T(8,128)(2,1)}, ...), condition=%wide.region_16.17_spmd.clone, body=%wide.region_15.16_spmd.clone.sunk | while | flops 1836290 | bytes 2642553 | solution.py:150
  107.2 0.6 broadcast_divide_fusion.3
  107.9 0.7 iota_compare_fusion.6
  108.5 2.9 %select_convert_fusion.7 = bf16[256,1024]{1,0:T(8,128)(2,1)} fusion(f32[256,1024]{1,0:T(8,128)S(1)} %get-tuple-element.872, f32[256,1024]{1,0:T(8,128)} %get-tuple-element.870, f32[]{:T(128)} %get-tuple-element.868, f32[1024]{0:T(1024)S(1)} %get-tuple-element.871, f32[1024]{0:T(1024)S(1)} %broadcast_divide_fusion.3, f32[1024]{0:T(1024)S(1)} %bitcast.37, ...), kind=kLoop, calls=%fused_computation.18.clone.1 | loop fusion | flops 1835008 | bytes 2633988 | tf_op jit(solution)/shard_map/while/body/convert_element_type | solution.py:145
  111.5 2.0 copy.22
  113.5 0.0 copy-done.8
  113.5 3.7 %all-to-all-start = ((bf16[256,16,64]{0,2,1:T(8,128)(2,1)}), bf16[256,16,64]{0,2,1:T(8,128)(2,1)S(1)}, u32[]{:S(2)}, u32[]{:S(2)}) async-start(bf16[256,16,64]{0,2,1:T(8,128)(2,1)} %bitcast.2), calls=%async_computation | async-start | bytes 1048576 | tf_op jit(solution)/shard_map/all_to_all | solution.py:30
  117.2 0.0 reduce-scatter.2.cloned.1.call-start
  117.3 0.7 reduce-scatter.2.cloned.1.call-update
  118.0 41.9 %all-gather = s32[32,1,256]{2,1,0:T(1,128)S(1)} all-gather(s32[1,1,256]{2,1,0:T(1,128)S(1)} %bitcast.41), channel_id=1, replica_groups=mesh['dp'=16,'rep'=2] {'dp','rep'}, dimensions={0}, use_global_device_ids=true | all-gather | bytes 33792 | tf_op jit(solution)/shard_map/all_gather | solution.py:36
  159.8 0.2 remainder_reduce_fusion
  160.1 0.0 all-to-all-done
  160.1 0.3 copy.23
  160.4 0.2 all_to_all.29
  160.6 0.0 copy-start.11
  160.6 0.0 copy-start.12
  160.7 4.2 %all_to_all.35 = bf16[4096,2,32]{0,2,1:T(8,128)(2,1)S(1)} all-to-all(bf16[4096,2,32]{0,2,1:T(8,128)(2,1)S(1)} %all_to_all.29), channel_id=1, replica_groups=mesh['dp'=16,'rep'=2] {'rep'}, dimensions={1} | all-to-all | bytes 1048576 | tf_op jit(solution)/shard_map/all_to_all | solution.py:29
  164.9 11.9 %fusion.16 = f32[32,512]{1,0:T(8,128)} fusion(bf16[8192,32]{0,1:T(8,128)(2,1)S(1)} %bitcast.35, s32[512]{0:T(512)S(1)} %copy-done.11, s32[8192]{0:T(1024)S(1)} %add_select_fusion.2, s32[512]{0:T(512)S(1)} %copy-done.12), kind=kOutput, calls=%fused_computation.30 | convolution fusion | flops 318767104 | bytes 626688 | tf_op jit(solution)/shard_map/while/body/eval_jaxpr/dot_general | solution.py:46
  176.8 81.1 %reduce-scatter.2.cloned.1.call-done = f32[32,128]{1,0:T(8,128)} async-done(((f32[1024,128]{1,0:T(8,128)}), f32[32,128]{1,0:T(8,128)}) %reduce-scatter.2.cloned.1.call-update) | async-done | bytes 16400 | tf_op jit(solution)/shard_map/reduce_scatter | solution.py:153
  (27 shorter events, 0.2 us)
Async XLA Ops:
  7.2 1.5 copy-start
  11.2 44.0 %copy-start.5 = (f32[1024]{0:T(1024)S(1)}, f32[1024]{0:T(1024)}, u32[]{:S(2)}) copy-start(f32[1024]{0:T(1024)} %param.21) | copy-start | bytes 12292
  12.3 45.4 %copy-start.1 = (f32[256,1024]{1,0:T(8,128)S(1)}, f32[256,1024]{1,0:T(8,128)}, u32[]{:S(2)}) copy-start(f32[256,1024]{1,0:T(8,128)} %get-tuple-element.789) | copy-start | bytes 3145732
  12.3 45.4 %copy-start.3 = (bf16[1024,128]{1,0:T(8,128)(2,1)S(1)}, bf16[1024,128]{1,0:T(8,128)(2,1)}, u32[]{:S(2)}) copy-start(bf16[1024,128]{1,0:T(8,128)(2,1)} %param.23) | copy-start | bytes 786436
  12.3 45.4 %copy-start.4 = (bf16[256,128]{1,0:T(8,128)(2,1)S(1)}, bf16[256,128]{1,0:T(8,128)(2,1)}, u32[]{:S(2)}) copy-start(bf16[256,128]{1,0:T(8,128)(2,1)} %param.25) | copy-start | bytes 196612
  12.3 45.4 %copy-start.6 = (f32[1024]{0:T(1024)S(1)}, f32[1024]{0:T(1024)}, u32[]{:S(2)}) copy-start(f32[1024]{0:T(1024)} %param.22) | copy-start | bytes 12292
  12.3 45.4 %copy-start.9 = (f32[128]{0:T(128)S(1)}, f32[128]{0:T(128)}, u32[]{:S(2)}) copy-start(f32[128]{0:T(128)} %param.24) | copy-start | bytes 1540
  62.7 44.5 %copy-start.2 = (f32[1024,128]{1,0:T(8,128)}, f32[1024,128]{1,0:T(8,128)S(1)}, u32[]{:S(2)}) copy-start(f32[1024,128]{1,0:T(8,128)S(1)} %get-tuple-element.395) | copy-start | bytes 1572868
  111.4 2.0 copy-start.7
  111.4 2.0 copy-start.8
  113.5 4.5 %copy-start.10 = (s32[256]{0:T(256)S(1)}, s32[256]{0:T(256)}, u32[]{:S(2)}) copy-start(s32[256]{0:T(256)} %param.16) | copy-start | bytes 3076
  113.5 46.6 %all-to-all-start = ((bf16[256,16,64]{0,2,1:T(8,128)(2,1)}), bf16[256,16,64]{0,2,1:T(8,128)(2,1)S(1)}, u32[]{:S(2)}, u32[]{:S(2)}) async-start(bf16[256,16,64]{0,2,1:T(8,128)(2,1)} %bitcast.2), calls=%async_computation | async-start | bytes 1048576 | tf_op jit(solution)/shard_map/all_to_all | solution.py:30
  117.2 140.7 %reduce-scatter.2.cloned.1.call-start = ((), (), s32[]{:S(2)}) async-start(), calls=%async_computation.3 | async-start | bytes 540672 | tf_op jit(solution)/shard_map/reduce_scatter | solution.py:153
  160.6 4.2 %copy-start.11 = (s32[512]{0:T(512)S(1)}, s32[512]{0:T(512)}, u32[]{:S(2)}) copy-start(s32[512]{0:T(512)} %param.19) | copy-start | bytes 6148
  160.6 4.2 %copy-start.12 = (s32[512]{0:T(512)S(1)}, s32[512]{0:T(512)}, u32[]{:S(2)}) copy-start(s32[512]{0:T(512)} %param.18) | copy-start | bytes 6148
Sparse Core Ops, SparseCore 0:
  120.8 137.0 reduce-scatter.1
